TPU v7x, 32 devices: a whole 2x2x4 slice. The times are simulated.
32 devices in a mesh: dp: 8 (over z, y), mp: 4 (over x, core).
Axes of the slice: x: 2, y: 2, z: 4, core: 2. Of those that a mesh axis runs over, the one named last changes fastest.
Arguments:
- gradients: bfloat16 [4, 16, 1024, 1024], P(None, 'mp', 'dp'), as said below
- statistics: float32 [4, 32, 1024, 1024], P('mp', 'dp'), as said below
- accumulator: float32 [4, 16, 1024, 1024], P(None, 'mp', 'dp'), may hold values from 0.25 to 4
Outputs:
- update: float32 [4, 16, 1024, 1024], P(None, 'mp', 'dp')
- statistics_new: float32 [4, 32, 1024, 1024], P('mp', 'dp')
- accumulator_new: float32 [4, 16, 1024, 1024], P(None, 'mp', 'dp')
Inputs may be any that keep to these rules, and one draw needn't show every extreme that they name: `gradients`: Real-valued gradient blocks. `statistics`: each 1024 x 1024 statistic is symmetric positive definite.
All inputs are finite; a program needn't handle non-finite values.
Results may differ from a plain program's by a relative error of at most 0.005.
The roundings to bfloat16 on the way count: a program that leaves them out, or rounds other values in their place, can miss the bound.
Values may be sent and summed in bfloat16 or wider, within the bound.
A program may use at most 192 MiB of HBM per device.

v0:
```python
import jax
import jax.numpy as jnp
from jax import lax
from jax.sharding import PartitionSpec as P

ITERS = 3


def partner_2(value, axis, distance):
    return lax.ppermute(value, axis, [(i, i ^ 1 << distance) for i in range(lax.axis_size(axis))])


def batch_dot(left, right):
    return jnp.einsum("kij,kjl->kil", left, right, preferred_element_type=jnp.float32)


def inverse_roots(statistic):
    block_width = statistic.shape[-1]
    identity = jnp.eye(block_width, dtype=jnp.float32)
    frob_norms = jnp.sqrt(jnp.sum(statistic * statistic, axis=(1, 2)) + 1e-06)
    newton_scale = (2.5 / frob_norms)[:, None, None]
    matrix = newton_scale * statistic
    root_iter = jnp.sqrt(jnp.sqrt(newton_scale)) * identity
    for iteration in range(ITERS):
        factor = (1.25 * identity - 0.25 * matrix).astype(jnp.bfloat16)
        root_iter = batch_dot(root_iter.astype(jnp.bfloat16), factor)
        if iteration + 1 < ITERS:
            square = batch_dot(factor, factor).astype(jnp.bfloat16)
            fourth = batch_dot(square, square).astype(jnp.bfloat16)
            matrix = batch_dot(fourth, matrix.astype(jnp.bfloat16))
    return root_iter


def on_device(gradients, statistics, accumulator):
    owners = lax.axis_size("dp")
    own_index = lax.axis_index("dp")
    row_blocks, col_blocks, dev_rows, block_width = gradients.shape
    blocks = row_blocks * col_blocks
    owned_factors = statistics.shape[1]
    split_pairs = owned_factors == 1
    half_rows = dev_rows // 2
    parity = own_index % 2
    left_side = parity == 0
    by_block = gradients.reshape(blocks, dev_rows, block_width)
    grads_wide = gradients.astype(jnp.float32)
    grad_total = lax.psum(jnp.sum(grads_wide * grads_wide), ("dp", "mp"))
    entries = blocks * dev_rows * block_width * owners * lax.axis_size("mp")
    clip_factor = jnp.minimum(1.0, jnp.sqrt(entries / (grad_total + 1e-06)))
    scaled = clip_factor * grads_wide
    accumulated = accumulator + scaled * scaled
    graft_step = scaled / jnp.sqrt(accumulated)
    graft_squares = jnp.sum(graft_step * graft_step)
    row_parts = 2 if split_pairs else 1
    row_units = by_block.reshape(blocks * row_parts, dev_rows // row_parts, block_width)
    received = lax.all_to_all(row_units, "dp", split_axis=0, concat_axis=1, tiled=True)
    if split_pairs:
        partner_part = partner_2(received, "dp", 0)
        own_part = received.reshape(owners, 1, half_rows, block_width)
        partner_part = partner_part.reshape(owners, 1, half_rows, block_width)
        ordered = jnp.where(
            left_side,
            jnp.concatenate([own_part, partner_part], 1),
            jnp.concatenate([partner_part, own_part], 1),
        )
        whole_blocks = ordered.reshape(1, owners * dev_rows, block_width)
    else:
        whole_blocks = received
    transposed = jnp.swapaxes(whole_blocks, 1, 2)
    if split_pairs:
        factor_inputs = jnp.where(left_side, whole_blocks, transposed)
    else:
        factor_inputs = jnp.stack([whole_blocks, transposed], 1).reshape(
            owned_factors, block_width, block_width
        )
    gram_matrix = jnp.einsum(
        "kij,klj->kil", factor_inputs, factor_inputs, preferred_element_type=jnp.float32
    )
    statistics_new = (
        0.9 * statistics[0] + 0.1 / block_width * clip_factor * clip_factor * gram_matrix
    )
    root_values = inverse_roots(statistics_new).astype(jnp.bfloat16)
    if split_pairs:
        partner = partner_2(root_values, "dp", 0)
        left_root = jnp.where(left_side, root_values, partner)[0]
        right_root = jnp.where(left_side, partner, root_values)[0]
        left_rows = lax.dynamic_slice_in_dim(
            left_root.reshape(owners, 2, half_rows, block_width), parity, 1, 1
        )
        left_rows = left_rows.reshape(owners * half_rows, block_width)
        left_applied = jnp.dot(
            left_rows, whole_blocks[0], preferred_element_type=jnp.float32
        ).astype(jnp.bfloat16)
        product = jnp.dot(left_applied, right_root, preferred_element_type=jnp.float32)
        pieces = product.reshape(1, owners, half_rows, block_width)
    else:
        root_pairs = root_values.reshape(-1, 2, block_width, block_width)
        left_applied = batch_dot(root_pairs[:, 0], whole_blocks).astype(jnp.bfloat16)
        product = batch_dot(left_applied, root_pairs[:, 1])
        pieces = product.reshape(-1, owners, dev_rows, block_width)
    returned = lax.all_to_all(
        pieces.astype(jnp.bfloat16), "dp", split_axis=1, concat_axis=0, tiled=True
    ).astype(pieces.dtype)
    returned = returned.reshape(row_blocks, col_blocks, dev_rows, block_width)
    graft_total, update_total = lax.psum(
        (graft_squares, jnp.sum(returned * returned)), ("dp", "mp")
    )
    graft_ratio = jnp.sqrt(graft_total / (update_total + 1e-06))
    return (graft_ratio * returned, statistics_new[None], accumulated)


def solution(mesh):
    return jax.shard_map(
        on_device,
        mesh=mesh,
        in_specs=(P(None, "mp", "dp", None), P("mp", "dp", None, None), P(None, "mp", "dp", None)),
        out_specs=(P(None, "mp", "dp", None), P("mp", "dp", None, None), P(None, "mp", "dp", None)),
        check_vma=False,
    )
```

profile of v0, /device:TPU:12, one launch (start us, length us, event | category | flops | bytes accessed | tf_op | source)
XLA Modules:
  0.0 485.6 jit_solution(2648131232850951314)
XLA Ops:
  0.6 6.2 %all-to-all-start = ((bf16[16,128,1024]{2,1,0:T(8,128)(2,1)}), bf16[16,128,1024]{2,1,0:T(8,128)(2,1)}, u32[]{:S(2)}, u32[]{:S(2)}) async-start(bf16[16,128,1024]{2,1,0:T(8,128)(2,1)} %bitcast.47), calls=%async_computation | async-start | bytes 8388608 | tf_op jit(solution)/shard_map/all_to_all | solution.py:55
  6.9 5.0 %fusion.5 = f32[]{:T(128)} fusion(bf16[4,4,128,1024]{3,2,1,0:T(8,128)(2,1)} %param.3), kind=kLoop, calls=%fused_computation.16 | loop fusion | flops 6291455 | bytes 4194308 | tf_op jit(solution)/shard_map/reduce_sum | solution.py:46
  11.8 107.4 %psum.21 = f32[]{:T(128)} all-reduce(f32[]{:T(128)} %fusion.5), channel_id=1, replica_groups=mesh['dp'=8,'mp'=4] {'dp','mp'}, use_global_device_ids=true, to_apply=%region_1.0 | all-reduce | flops 1 | bytes 8 | tf_op jit(solution)/shard_map/psum | solution.py:46
  120.0 2.5 fusion.33
  122.4 2.4 fusion.34
  124.9 0.0 all-to-all-done
  124.9 6.7 %copy.10 = bf16[8,2,128,1024]{2,0,3,1:T(8,128)(2,1)} copy(bf16[8,2,128,1024]{3,2,1,0:T(8,128)(2,1)} %bitcast.2) | data formatting | bytes 8388608 | tf_op jit(solution)/shard_map/all_to_all | solution.py:55
  131.6 7.3 %all_to_all.23 = bf16[2,1024,1024]{1,2,0:T(8,128)(2,1)} reshape(bf16[2,8,128,1024]{2,1,3,0:T(8,128)(2,1)} %bitcast.48) | data formatting | bytes 8388608 | tf_op jit(solution)/shard_map/all_to_all | solution.py:55
  139.0 0.0 copy-start
  139.0 5.0 %copy.11 = bf16[2,8,128,1024]{3,2,1,0:T(8,128)(2,1)} copy(bf16[2,8,128,1024]{3,2,0,1:T(8,128)(2,1)} %bitcast.4) | data formatting | bytes 8388608 | tf_op jit(solution)/shard_map/all_to_all | solution.py:55
  143.9 0.0 copy-done
  143.9 6.3 %pad_maximum_fusion = bf16[2,2,1024,1024]{3,2,1,0:T(8,128)(2,1)} fusion(bf16[2,1,1024,1024]{3,2,1,0:T(8,128)(2,1)S(1)} %bitcast.49, bf16[2,1,1024,1024]{3,2,1,0:T(8,128)(2,1)} %bitcast.50), kind=kLoop, calls=%fused_computation.20 | loop fusion | flops 4194304 | bytes 16777216 | tf_op jit(solution)/shard_map/stack | solution.py:72
  150.3 22.7 %multiply_reduce_fusion = (f32[4]{0:T(128)S(1)}, f32[4,1024,1024]{2,1,0:T(8,128)}) fusion(bf16[4,1024,1024]{2,1,0:T(8,128)(2,1)} %bitcast.52, f32[]{:T(128)S(6)} %mul.104, f32[1,4,1024,1024]{3,2,1,0:T(8,128)} %param.4), kind=kOutput, calls=%fused_computation.5 | convolution fusion | flops 8610906112 | bytes 41943060 | tf_op jit(solution)/shard_map/kij,klj->kil/dot_general | solution.py:75
  172.9 22.1 %fusion.46 = bf16[4,1024,1024]{2,1,0:T(8,128)(2,1)} fusion(f32[4,1024,1024]{2,1,0:T(8,128)} %get-tuple-element.10, f32[4]{0:T(128)S(1)} %get-tuple-element.8, f32[1024,1024]{1,0:T(8,128)} %fusion.33), kind=kOutput, calls=%fused_computation.50 | convolution fusion | flops 8606711808 | bytes 29360144 | tf_op jit(solution)/shard_map/kij,kjl->kil/dot_general | solution.py:14
  195.0 24.0 %fusion.7 = f32[4,1024,1024]{2,1,0:T(8,128)} fusion(f32[4,1024,1024]{2,1,0:T(8,128)} %get-tuple-element.10, bf16[4,1024,1024]{2,1,0:T(8,128)(2,1)} %fusion.46, f32[4]{0:T(128)S(1)} %get-tuple-element.8), kind=kOutput, calls=%fused_computation.18 | convolution fusion | flops 17192452096 | bytes 41943056 | tf_op jit(solution)/shard_map/kij,kjl->kil/dot_general | solution.py:14
  219.0 21.3 %fusion.42 = bf16[4,1024,1024]{2,1,0:T(8,128)(2,1)} fusion(f32[4,1024,1024]{2,1,0:T(8,128)} %fusion.7, f32[1024,1024]{1,0:T(8,128)} %fusion.33), kind=kOutput, calls=%fused_computation.45 | convolution fusion | flops 8602517504 | bytes 29360128 | tf_op jit(solution)/shard_map/kij,kjl->kil/dot_general | solution.py:14
  240.3 28.1 %subtract_convert_fusion = bf16[4,1024,1024]{2,1,0:T(8,128)(2,1)} fusion(f32[4,1024,1024]{2,1,0:T(8,128)} %fusion.7, bf16[4,1024,1024]{2,1,0:T(8,128)(2,1)} %fusion.42, f32[1024,1024]{1,0:T(8,128)} %fusion.33), kind=kOutput, calls=%fused_computation.1 | convolution fusion | flops 17200840704 | bytes 37748736 | tf_op jit(solution)/shard_map/kij,kjl->kil/dot_general | solution.py:14
  268.4 19.1 %fusion.8 = bf16[4,1024,1024]{2,1,0:T(8,128)(2,1)} fusion(f32[1024,1024]{1,0:T(8,128)} %fusion.34, f32[4]{0:T(128)S(1)} %get-tuple-element.7, f32[4,1024,1024]{2,1,0:T(8,128)} %get-tuple-element.10, f32[4]{0:T(128)S(1)} %get-tuple-element.8, f32[1024,1024]{1,0:T(8,128)} %fusion.33), kind=kOutput, calls=%fused_computation.19 | convolution fusion | flops 8615100416 | bytes 33554464 | tf_op jit(solution)/shard_map/kij,kjl->kil/dot_general | solution.py:14
  287.4 28.1 %fusion.27 = bf16[4,1024,1024]{2,1,0:T(8,128)(2,1)} fusion(bf16[4,1024,1024]{2,1,0:T(8,128)(2,1)} %subtract_convert_fusion, bf16[4,1024,1024]{2,1,0:T(8,128)(2,1)} %fusion.8, f32[4,1024,1024]{2,1,0:T(8,128)} %fusion.7, f32[1024,1024]{1,0:T(8,128)} %fusion.33), kind=kOutput, calls=%fused_computation.35 | convolution fusion | flops 17200840704 | bytes 46137344 | tf_op jit(solution)/shard_map/kij,kjl->kil/dot_general | solution.py:14
  315.5 13.3 %fusion.39 = bf16[2,1024,1024]{2,1,0:T(8,128)(2,1)} fusion(bf16[2,2,1024,1024]{3,2,1,0:T(8,128)(2,1)} %bitcast.55, bf16[2,1024,1024]{1,2,0:T(8,128)(2,1)} %all_to_all.23), kind=kOutput, calls=%fused_computation.44 | convolution fusion | flops 8594128896 | bytes 16777216 | tf_op jit(solution)/shard_map/kij,kjl->kil/dot_general | solution.py:14
  328.8 4.8 copy.13
  333.6 6.5 %all-to-all-start.1 = ((bf16[2,8,128,1024]{3,2,0,1:T(8,128)(2,1)}), bf16[2,8,128,1024]{3,2,0,1:T(8,128)(2,1)}, u32[]{:S(2)}, u32[]{:S(2)}) async-start(bf16[2,8,128,1024]{3,2,0,1:T(8,128)(2,1)} %copy.13), calls=%async_computation.1 | async-start | bytes 8388608 | tf_op jit(solution)/shard_map/all_to_all | solution.py:100
  340.1 8.4 %fusion.4 = (f32[]{:T(128)}, f32[4,4,128,1024]{3,2,1,0:T(8,128)}) fusion(bf16[4,4,128,1024]{3,2,1,0:T(8,128)(2,1)} %param.3, f32[]{:T(128)S(6)} %min_shard_map.3, f32[4,4,128,1024]{3,2,1,0:T(8,128)} %param.5), kind=kLoop, calls=%fused_computation.15 | loop fusion | flops 14680063 | bytes 20971528 | tf_op jit(solution)/shard_map/reduce_sum | solution.py:52
  348.5 80.1 %all-to-all-done.1 = bf16[2,8,128,1024]{3,2,0,1:T(8,128)(2,1)} async-done(((bf16[2,8,128,1024]{3,2,0,1:T(8,128)(2,1)}), bf16[2,8,128,1024]{3,2,0,1:T(8,128)(2,1)}, u32[]{:S(2)}, u32[]{:S(2)}) %all-to-all-start.1) | async-done | bytes 4194336 | tf_op jit(solution)/shard_map/all_to_all | solution.py:100
  428.6 5.0 %fusion.6 = f32[]{:T(128)} fusion(bf16[2,8,128,1024]{3,2,0,1:T(8,128)(2,1)} %all-to-all-done.1), kind=kLoop, calls=%fused_computation.17 | loop fusion | flops 6291455 | bytes 4194308 | tf_op jit(solution)/shard_map/reduce_sum | solution.py:105
  433.6 43.9 %all-reduce = (f32[]{:T(128)}, f32[]{:T(128)}) all-reduce(f32[]{:T(128)} %get-tuple-element.5, f32[]{:T(128)} %fusion.6), channel_id=1, replica_groups=mesh['dp'=8,'mp'=4] {'dp','mp'}, use_global_device_ids=true, to_apply=%region_3.0 | all-reduce | flops 2 | bytes 16 | tf_op jit(solution)/shard_map/psum | solution.py:104
  478.8 6.8 %convert_multiply_fusion = f32[2,8,128,1024]{3,2,0,1:T(8,128)} fusion(bf16[2,8,128,1024]{3,2,0,1:T(8,128)(2,1)} %all-to-all-done.1, f32[]{:T(128)S(6)} %sqrt.33), kind=kLoop, calls=%fused_computation.7 | loop fusion | flops 4194304 | bytes 12582916 | tf_op jit(solution)/shard_map/mul | solution.py:108
  (1 shorter events, 0.0 us)
Async XLA Ops:
  0.6 124.3 %all-to-all-start = ((bf16[16,128,1024]{2,1,0:T(8,128)(2,1)}), bf16[16,128,1024]{2,1,0:T(8,128)(2,1)}, u32[]{:S(2)}, u32[]{:S(2)}) async-start(bf16[16,128,1024]{2,1,0:T(8,128)(2,1)} %bitcast.47), calls=%async_computation | async-start | bytes 8388608 | tf_op jit(solution)/shard_map/all_to_all | solution.py:55
  139.0 5.0 %copy-start = (bf16[2,1024,1024]{1,2,0:T(8,128)(2,1)S(1)}, bf16[2,1024,1024]{1,2,0:T(8,128)(2,1)}, u32[]{:S(2)}) copy-start(bf16[2,1024,1024]{1,2,0:T(8,128)(2,1)} %all_to_all.23) | copy-start | bytes 12582916
  333.6 95.0 %all-to-all-start.1 = ((bf16[2,8,128,1024]{3,2,0,1:T(8,128)(2,1)}), bf16[2,8,128,1024]{3,2,0,1:T(8,128)(2,1)}, u32[]{:S(2)}, u32[]{:S(2)}) async-start(bf16[2,8,128,1024]{3,2,0,1:T(8,128)(2,1)} %copy.13), calls=%async_computation.1 | async-start | bytes 8388608 | tf_op jit(solution)/shard_map/all_to_all | solution.py:100
where the time goes:
time: 487 us; the launch traced here: 486 us
  matrix products  179 us (37%)
  blocking collectives  151 us (31%)
  waiting for transfers between devices  80.1 us (16%)
  other arithmetic  36.4 us (7%)
  local copies, waits for them, and re-layouts  23.8 us (5%)
  starting transfers between devices  12.8 us (3%)
    dot_general x7, matrix products, batch_dot(): jnp.einsum('kij,kjl->kil', left, right, preferred_element_type=jnp.float32)  156 us
    psum x1, blocking collectives, on_device(): grad_total = lax.psum(jnp.sum(grads_wide * grads_wide), ('dp', 'mp'))  107 us
    all_to_all x1, waiting for transfers between devices, on_device(): lax.all_to_all(pieces.astype(jnp.bfloat16), 'dp', split_axis=1, concat_ax...  80.1 us
    psum x1, blocking collectives, on_device(): lax.psum((graft_squares, jnp.sum(returned * returned)), ('dp', 'mp'))  43.9 us
    dot_general x1, matrix products, on_device(): jnp.einsum('kij,klj->kil', factor_inputs, factor_inputs, preferred_elemen...  22.7 us
    all_to_all x3, local copies, waits for them, and re-layouts, on_device(): lax.all_to_all(row_units, 'dp', split_axis=0, concat_axis=1, tiled=True)  19 us
  transfers between devices with their start and end apart: 2, of which 1 were waited for; matrix products, arithmetic and copies ran while one was open for 4% of the time, Pallas kernels for 0%

commit v1 on v0

--- a/solution.py
+++ b/solution.py
@@ -1,6 +1,8 @@
 import jax
 import jax.numpy as jnp
 from jax import lax
+from jax.experimental import pallas as pl
+from jax.experimental.pallas import tpu as pltpu
 from jax.sharding import PartitionSpec as P
 
 ITERS = 3
@@ -31,7 +33,7 @@
     return root_iter
 
 
-def on_device(gradients, statistics, accumulator):
+def split_device(gradients, statistics, accumulator):
     owners = lax.axis_size("dp")
     own_index = lax.axis_index("dp")
     row_blocks, col_blocks, dev_rows, block_width = gradients.shape
@@ -108,6 +110,234 @@
     return (graft_ratio * returned, statistics_new[None], accumulated)
 
 
+TILE = 512
+CHUNK = 128
+
+
+def refresh_kernel(slot, width, aliased, *refs):
+    scale_ref, grad_hbm, stats_hbm = refs[:3]
+    refs = refs[4:] if aliased else refs[3:]
+    out_stats, product_ref, sum_ref = refs[:3]
+    stat, pair, fr, sqr, fourth, mats, frob, in_sem, out_sem, grad_sem = refs[3:]
+    tile = min(TILE, width)
+    tiles = width // tile
+    dot = lambda a, b: jnp.dot(a, b, preferred_element_type=jnp.float32)
+
+    grad_copy = pltpu.make_async_copy(grad_hbm, pair.at[0], grad_sem)
+    grad_copy.start()
+    loads = [
+        pltpu.make_async_copy(stats_hbm.at[2 * slot + s], stat.at[s], in_sem.at[s])
+        for s in range(2)
+    ]
+    for load in loads:
+        load.start()
+    grad_copy.wait()
+
+    @pl.loop(0, width // CHUNK)
+    def _(i):
+        rows = pl.ds(pl.multiple_of(i * CHUNK, CHUNK), CHUNK)
+        pair[1, :, rows] = pair[0, rows, :].T
+
+    def over_tiles(count, body):
+        @pl.loop(0, count * tiles)
+        def _(i):
+            body(i // tiles, pl.multiple_of(lax.rem(i, tiles) * tile, tile))
+
+    def diagonal(row, rows):
+        row_ids = lax.broadcasted_iota(jnp.int32, (rows, width), 0) + row
+        return row_ids == lax.broadcasted_iota(jnp.int32, (rows, width), 1)
+
+    scale = scale_ref[0]
+    stores = [
+        pltpu.make_async_copy(stat.at[s], out_stats.at[2 * slot + s], out_sem.at[s])
+        for s in range(2)
+    ]
+    for s in range(2):
+        loads[s].wait()
+        frob[s] = jnp.zeros((8, width), jnp.float32)
+
+        def gram(_, row, s=s):
+            rows = pl.ds(row, tile)
+            new = 0.9 * stat[s, rows, :] + scale * dot(pair[s, rows, :], pair[1 - s])
+            stat[s, rows, :] = new
+            frob[s] += jnp.sum((new * new).reshape(tile // 8, 8, width), axis=0)
+
+        over_tiles(1, gram)
+        stores[s].start()
+
+    for s in range(2):
+        total = jnp.sum(jnp.sum(frob[s], axis=0, keepdims=True), axis=1, keepdims=True)
+        newton_scale = 2.5 / jnp.sqrt(total + 1e-06)
+        first_root = jnp.sqrt(jnp.sqrt(newton_scale)).astype(jnp.bfloat16).astype(jnp.float32)
+
+        @pl.loop(0, width // CHUNK)
+        def _(i, s=s, newton_scale=newton_scale, first_root=first_root):
+            row = pl.multiple_of(i * CHUNK, CHUNK)
+            rows = pl.ds(row, CHUNK)
+            matrix = newton_scale * stat[s, rows, :]
+            quarter = -0.25 * matrix
+            factor = jnp.where(diagonal(row, CHUNK), 1.25 + quarter, quarter)
+            factor = factor.astype(jnp.bfloat16)
+            fr[s, 0, rows, :] = factor
+            fr[s, 1, rows, :] = (first_root * factor.astype(jnp.float32)).astype(jnp.bfloat16)
+            mats[0, s, rows, :] = matrix.astype(jnp.bfloat16)
+
+    def square(s, row):
+        rows = pl.ds(row, tile)
+        sqr[s, 0, rows, :] = dot(fr[s, 0, rows, :], fr[s, 0]).astype(jnp.bfloat16)
+
+    def square_and_root(j, row):
+        s, kind = j // 2, lax.rem(j, 2)
+        rows = pl.ds(row, tile)
+        sqr[s, kind, rows, :] = dot(fr[s, kind, rows, :], fr[s, 0]).astype(jnp.bfloat16)
+
+    def power(s, row):
+        rows = pl.ds(row, tile)
+        fourth[s, rows, :] = dot(sqr[s, 0, rows, :], sqr[s, 0]).astype(jnp.bfloat16)
+
+    def next_matrix(step):
+        def body(s, row):
+            rows = pl.ds(row, tile)
+            matrix = dot(fourth[s, rows, :], mats[step, s])
+            quarter = -0.25 * matrix
+            factor = jnp.where(diagonal(row, tile), 1.25 + quarter, quarter)
+            fr[s, 0, rows, :] = factor.astype(jnp.bfloat16)
+            if step + 2 < ITERS:
+                mats[step + 1, s, rows, :] = matrix.astype(jnp.bfloat16)
+
+        return body
+
+    over_tiles(2, square)
+    for step in range(ITERS - 1):
+        if step:
+            over_tiles(4, square_and_root)
+        over_tiles(2, power)
+        over_tiles(2, next_matrix(step))
+
+    def last_root(s, row):
+        rows = pl.ds(row, tile)
+        fr[s, 1, rows, :] = dot(sqr[s, 1, rows, :], fr[s, 0]).astype(jnp.bfloat16)
+
+    over_tiles(2, last_root)
+
+    def apply_left(_, row):
+        rows = pl.ds(row, tile)
+        pair[1, rows, :] = dot(fr[0, 1, rows, :], pair[0]).astype(jnp.bfloat16)
+
+    over_tiles(1, apply_left)
+    frob[0] = jnp.zeros((8, width), jnp.float32)
+
+    def apply_right(_, row):
+        rows = pl.ds(row, tile)
+        product = dot(pair[1, rows, :], fr[1, 1])
+        product_ref[rows, :] = product.astype(jnp.bfloat16)
+        frob[0] += jnp.sum((product * product).reshape(tile // 8, 8, width), axis=0)
+
+    over_tiles(1, apply_right)
+    sum_ref[...] = frob[0]
+    for store in stores:
+        store.wait()
+
+
+def refresh_block(slot, scale, block, statistics, previous):
+    width = block.shape[-1]
+    aliased = previous is not None
+    hbm = pl.BlockSpec(memory_space=pl.ANY)
+    vmem = pl.BlockSpec(memory_space=pltpu.VMEM)
+    operands = (scale.reshape(1), block, statistics) + ((previous,) if aliased else ())
+    return pl.pallas_call(
+        lambda *refs: refresh_kernel(slot, width, aliased, *refs),
+        out_shape=(
+            jax.ShapeDtypeStruct(statistics.shape, jnp.float32),
+            jax.ShapeDtypeStruct((width, width), jnp.bfloat16),
+            jax.ShapeDtypeStruct((8, width), jnp.float32),
+        ),
+        in_specs=[pl.BlockSpec(memory_space=pltpu.SMEM)] + [hbm] * (len(operands) - 1),
+        out_specs=(hbm, vmem, vmem),
+        scratch_shapes=[
+            pltpu.VMEM((2, width, width), jnp.float32),
+            pltpu.VMEM((2, width, width), jnp.bfloat16),
+            pltpu.VMEM((2, 2, width, width), jnp.bfloat16),
+            pltpu.VMEM((2, 2, width, width), jnp.bfloat16),
+            pltpu.VMEM((2, width, width), jnp.bfloat16),
+            pltpu.VMEM((2, 2, width, width), jnp.bfloat16),
+            pltpu.VMEM((2, 8, width), jnp.float32),
+            pltpu.SemaphoreType.DMA((2,)),
+            pltpu.SemaphoreType.DMA((2,)),
+            pltpu.SemaphoreType.DMA,
+        ],
+        input_output_aliases={3: 0} if aliased else {},
+        compiler_params=pltpu.CompilerParams(vmem_limit_bytes=56 * 2**20),
+        cost_estimate=pl.CostEstimate(
+            flops=40 * width**3, bytes_accessed=20 * width**2, transcendentals=0
+        ),
+        name=f"refresh_{slot}",
+    )(*operands)
+
+
+def finish_kernel(ratio_ref, *refs):
+    out_ref = refs[-1]
+    for slot, ref in enumerate(refs[:-1]):
+        out_ref[0, slot] = ratio_ref[0] * ref[0].astype(jnp.float32)
+
+
+def finish(ratio, returned):
+    owners, dev_rows, width = returned[0].shape
+    slots = len(returned)
+    return pl.pallas_call(
+        finish_kernel,
+        grid=(owners,),
+        out_shape=jax.ShapeDtypeStruct((owners, slots, dev_rows, width), jnp.float32),
+        in_specs=[pl.BlockSpec(memory_space=pltpu.SMEM)]
+        + [pl.BlockSpec((1, dev_rows, width), lambda i: (i, 0, 0))] * slots,
+        out_specs=pl.BlockSpec((1, slots, dev_rows, width), lambda i: (i, 0, 0, 0)),
+        name="finish",
+    )(ratio.reshape(1), *returned)
+
+
+def on_device(gradients, statistics, accumulator):
+    owned_factors = statistics.shape[1]
+    if owned_factors % 2:
+        return split_device(gradients, statistics, accumulator)
+    owners = lax.axis_size("dp")
+    row_blocks, col_blocks, dev_rows, block_width = gradients.shape
+    blocks = row_blocks * col_blocks
+    slots = owned_factors // 2
+    units = gradients.reshape(owners, slots, dev_rows, block_width)
+    exchange = lambda rows: lax.all_to_all(rows, "dp", 0, 0, tiled=True)
+    received = [exchange(units[:, 0])]
+    grads_wide = gradients.astype(jnp.float32)
+    grad_total = lax.psum(jnp.sum(grads_wide * grads_wide), ("dp", "mp"))
+    entries = blocks * dev_rows * block_width * owners * lax.axis_size("mp")
+    clip_factor = jnp.minimum(1.0, jnp.sqrt(entries / (grad_total + 1e-06)))
+    scale = 0.1 / block_width * clip_factor * clip_factor
+    for slot in range(1, slots):
+        later, _ = lax.optimization_barrier((units[:, slot], scale))
+        received.append(exchange(later))
+    statistics_new = None
+    returned = []
+    update_squares = 0.0
+    for slot in range(slots):
+        whole_block = received[slot].reshape(block_width, block_width)
+        statistics_new, product, squares = refresh_block(
+            slot, scale, whole_block, statistics[0], statistics_new
+        )
+        update_squares = update_squares + jnp.sum(squares)
+        returned.append(exchange(product.reshape(owners, dev_rows, block_width)))
+    late_gradients, late_accumulator, update_squares = lax.optimization_barrier(
+        (gradients, accumulator, update_squares)
+    )
+    scaled = clip_factor * late_gradients.astype(jnp.float32)
+    accumulated = late_accumulator + scaled * scaled
+    graft_step = scaled / jnp.sqrt(accumulated)
+    graft_total, update_total = lax.psum(
+        (jnp.sum(graft_step * graft_step), update_squares), ("dp", "mp")
+    )
+    graft_ratio = jnp.sqrt(graft_total / (update_total + 1e-06))
+    update = finish(graft_ratio, returned).reshape(gradients.shape)
+    return (update, statistics_new[None], accumulated)
+
+
 def solution(mesh):
     return jax.shard_map(
         on_device,

time: 487 us -> 296 us (0.61)
  matrix products: 179 us -> 0 us
  Pallas kernels: 0 us -> 128 us
  waiting for transfers between devices: 80.1 us -> 0.01 us
  blocking collectives: 151 us -> 116 us
  other arithmetic: 36.4 us -> 15.4 us
  local copies, waits for them, and re-layouts: 23.8 us -> 4.86 us
  starting transfers between devices: 12.8 us -> 24.8 us
    dot_general x8 -> x0, matrix products: 179 us -> none  [the longest x7 156 us: batch_dot(): jnp.einsum('kij,kjl->kil', left, right, preferred_element_type=jnp.float32)]
    pallas_call x0 -> x3, Pallas kernels: none -> 128 us  [the longest x2 121 us: refresh_block(): pl.pallas_call(lambda *refs: refresh_kernel(slot, width, aliased, *refs),...]
    all_to_all x2 -> x4, waiting for transfers between devices: 80.1 us -> 0.01 us  [on_device(): exchange = lambda rows: lax.all_to_all(rows, 'dp', 0, 0, tiled=True)]
    psum x1, blocking collectives: 107 us -> 62.5 us  [on_device(): grad_total = lax.psum(jnp.sum(grads_wide * grads_wide), ('dp', 'mp'))]
    all_to_all x3 -> x0, local copies, waits for them, and re-layouts: 19 us -> none  [on_device(): lax.all_to_all(row_units, 'dp', split_axis=0, concat_axis=1, tiled=True)]
    all_to_all x2 -> x4, starting transfers between devices: 12.8 us -> 24.8 us  [on_device(): exchange = lambda rows: lax.all_to_all(rows, 'dp', 0, 0, tiled=True)]
    psum x1, blocking collectives: 43.9 us -> 53.8 us  [on_device(): lax.psum((jnp.sum(graft_step * graft_step), update_squares), ('dp', 'mp'))]
    mul x2 -> x0, other arithmetic: 9.25 us -> none  [the longest x1 6.79 us: on_device(): return (graft_ratio * returned, statistics_new[None], accumulated)]
  transfers between devices with their start and end apart: 2 -> 4, of which waited for: 1 -> 0; matrix products, arithmetic and copies ran while one was open for 4% -> 5% of each run, Pallas kernels for 0% -> 41%
where the time goes in v1:
time: 296 us; the launch traced here: 294 us
  Pallas kernels  128 us (43%)
  blocking collectives  116 us (39%)
  starting transfers between devices  24.8 us (8%)
  other arithmetic  15.4 us (5%)
  local copies, waits for them, and re-layouts  4.86 us (2%)
  between operations  4.02 us (1%)
    pallas_call x2, Pallas kernels, refresh_block(): pl.pallas_call(lambda *refs: refresh_kernel(slot, width, aliased, *refs),...  121 us
    psum x1, blocking collectives, on_device(): grad_total = lax.psum(jnp.sum(grads_wide * grads_wide), ('dp', 'mp'))  62.5 us
    psum x1, blocking collectives, on_device(): lax.psum((jnp.sum(graft_step * graft_step), update_squares), ('dp', 'mp'))  53.8 us
    all_to_all x4, starting transfers between devices, on_device(): exchange = lambda rows: lax.all_to_all(rows, 'dp', 0, 0, tiled=True)  24.8 us
    reduce_sum x1, other arithmetic, on_device(): jnp.sum(graft_step * graft_step)  8.42 us
    pallas_call x1, Pallas kernels, finish(): pl.pallas_call(finish_kernel, grid=(owners,), out_shape=jax.ShapeDtypeStr...  7.22 us
  transfers between devices with their start and end apart: 4, of which 0 were waited for; matrix products, arithmetic and copies ran while one was open for 5% of the time, Pallas kernels for 41%

profile of v1, /device:TPU:12, one launch (start us, length us, event | category | flops | bytes accessed | tf_op | source)
XLA Modules:
  0.0 293.5 jit_solution(12613373818363764326)
XLA Ops:
  0.6 4.8 %slice_bitcast_fusion = (bf16[8,128,1024]{2,1,0:T(8,128)(2,1)}, bf16[8,128,1024]{2,1,0:T(8,128)(2,1)}) fusion(bf16[8,2,128,1024]{3,2,1,0:T(8,128)(2,1)} %bitcast.18), kind=kLoop, calls=%fused_computation.4 | loop fusion | bytes 8388608 | tf_op jit(solution)/shard_map/squeeze | solution.py:315
  5.5 6.2 %all-to-all-start = ((bf16[8,128,1024]{2,1,0:T(8,128)(2,1)}), bf16[8,128,1024]{2,1,0:T(8,128)(2,1)S(1)}, u32[]{:S(2)}, u32[]{:S(2)}) async-start(bf16[8,128,1024]{2,1,0:T(8,128)(2,1)} %get-tuple-element.28), calls=%async_computation | async-start | bytes 4194304 | tf_op jit(solution)/shard_map/all_to_all | solution.py:307
  11.7 4.9 %multiply_reduce_fusion.1 = f32[]{:T(128)} fusion(bf16[4,4,128,1024]{3,2,1,0:T(8,128)(2,1)} %param.3), kind=kLoop, calls=%fused_computation.3 | loop fusion | flops 6291455 | bytes 4194308 | tf_op jit(solution)/shard_map/reduce_sum | solution.py:310
  16.6 62.5 %psum.21 = f32[]{:T(128)} all-reduce(f32[]{:T(128)} %multiply_reduce_fusion.1), channel_id=1, replica_groups=mesh['dp'=8,'mp'=4] {'dp','mp'}, use_global_device_ids=true, to_apply=%region_1.0 | all-reduce | flops 1 | bytes 8 | tf_op jit(solution)/shard_map/psum | solution.py:310
  79.9 0.0 all-to-all-done
  79.9 0.0 copy-start.1
  79.9 6.6 %all-to-all-start.1 = ((bf16[8,128,1024]{2,1,0:T(8,128)(2,1)}), bf16[8,128,1024]{2,1,0:T(8,128)(2,1)}, u32[]{:S(2)}, u32[]{:S(2)}) async-start(bf16[8,128,1024]{2,1,0:T(8,128)(2,1)} %get-tuple-element.14), calls=%async_computation.1 | async-start | bytes 4194304 | tf_op jit(solution)/shard_map/all_to_all | solution.py:307
  86.4 0.0 copy-done.1
  86.4 60.5 %refresh_0.1 = (f32[4,1024,1024]{2,1,0:T(8,128)}, bf16[1024,1024]{1,0:T(8,128)(2,1)}, f32[8,1024]{1,0:T(8,128)}) custom-call(f32[1]{0:T(128)} %bitcast.refs_0_, bf16[1024,1024]{1,0:T(8,128)(2,1)} %bitcast.21, f32[4,1024,1024]{2,1,0:T(8,128)} %bitcast.23), custom_call_target="tpu_custom_call" | custom-call | flops 42949672960 | bytes 20971520 | tf_op jit(solution)/shard_map/refresh_0/pallas_call | solution.py:248
  146.9 0.0 all-to-all-done.1
  146.9 6.0 %all-to-all-start.2 = ((bf16[8,128,1024]{2,1,0:T(8,128)(2,1)}), bf16[8,128,1024]{2,1,0:T(8,128)(2,1)S(1)}, u32[]{:S(2)}, u32[]{:S(2)}) async-start(bf16[8,128,1024]{2,1,0:T(8,128)(2,1)} %bitcast.22), calls=%async_computation.2 | async-start | bytes 4194304 | tf_op jit(solution)/shard_map/all_to_all | solution.py:307
  152.9 0.0 copy-start.2
  152.9 60.5 %refresh_1.1 = (f32[4,1024,1024]{2,1,0:T(8,128)}, bf16[1024,1024]{1,0:T(8,128)(2,1)}, f32[8,1024]{1,0:T(8,128)}) custom-call(f32[1]{0:T(128)} %bitcast.refs_0_, bf16[1024,1024]{1,0:T(8,128)(2,1)} %bitcast.6.refs_1_, f32[4,1024,1024]{2,1,0:T(8,128)} %bitcast.24, f32[4,1024,1024]{2,1,0:T(8,128)} %get-tuple-element.15.refs_3_), custom_call_target="tpu_custom_call", output_to_operand_aliasing={{0}: (3, {})} | custom-call | flops 42949672960 | bytes 20971520 | tf_op jit(solution)/shard_map/refresh_1/pallas_call | solution.py:248
  213.4 0.0 all-to-all-done.2.refs_0_
  213.4 0.0 copy-start
  213.4 6.0 %all-to-all-start.3 = ((bf16[8,128,1024]{2,1,0:T(8,128)(2,1)}), bf16[8,128,1024]{2,1,0:T(8,128)(2,1)}, u32[]{:S(2)}, u32[]{:S(2)}) async-start(bf16[8,128,1024]{2,1,0:T(8,128)(2,1)} %bitcast.20), calls=%async_computation.3 | async-start | bytes 4194304 | tf_op jit(solution)/shard_map/all_to_all | solution.py:307
  219.5 0.0 copy-done.2
  219.5 0.6 reduce_sum.37
  220.1 1.4 reduce_sum.38
  222.7 8.4 %multiply_reduce_fusion = (f32[]{:T(128)}, f32[4,4,128,1024]{3,2,1,0:T(8,128)}) fusion(bf16[4,4,128,1024]{3,2,1,0:T(8,128)(2,1)} %param.3, f32[]{:T(128)S(6)} %min_shard_map.3, f32[4,4,128,1024]{3,2,1,0:T(8,128)} %param.5), kind=kLoop, calls=%fused_computation | loop fusion | flops 14680063 | bytes 20971528 | tf_op jit(solution)/shard_map/reduce_sum | solution.py:334
  231.1 0.0 copy-done
  231.1 53.8 %all-reduce = (f32[]{:T(128)}, f32[]{:T(128)}) all-reduce(f32[]{:T(128)} %get-tuple-element.25, f32[]{:T(128)S(6)} %add.19), channel_id=1, replica_groups=mesh['dp'=8,'mp'=4] {'dp','mp'}, use_global_device_ids=true, to_apply=%region_5.0 | all-reduce | flops 2 | bytes 16 | tf_op jit(solution)/shard_map/psum | solution.py:333
  286.3 0.0 all-to-all-done.3.refs_1_
  286.3 7.2 %finish.1 = f32[8,2,128,1024]{3,2,1,0:T(8,128)} custom-call(f32[1]{0:T(128)} %bitcast.7.ratio_ref, bf16[8,128,1024]{2,1,0:T(8,128)(2,1)} %copy-done, bf16[8,128,1024]{2,1,0:T(8,128)(2,1)} %all-to-all-done.3.refs_1_), custom_call_target="tpu_custom_call" | custom-call | tf_op jit(solution)/shard_map/finish/pallas_call | solution.py:287
Async XLA Ops:
  5.5 74.4 %all-to-all-start = ((bf16[8,128,1024]{2,1,0:T(8,128)(2,1)}), bf16[8,128,1024]{2,1,0:T(8,128)(2,1)S(1)}, u32[]{:S(2)}, u32[]{:S(2)}) async-start(bf16[8,128,1024]{2,1,0:T(8,128)(2,1)} %get-tuple-element.28), calls=%async_computation | async-start | bytes 4194304 | tf_op jit(solution)/shard_map/all_to_all | solution.py:307
  79.9 6.6 %copy-start.1 = (bf16[8,128,1024]{2,1,0:T(8,128)(2,1)}, bf16[8,128,1024]{2,1,0:T(8,128)(2,1)S(1)}, u32[]{:S(2)}) copy-start(bf16[8,128,1024]{2,1,0:T(8,128)(2,1)S(1)} %all-to-all-done) | copy-start | bytes 6291460
  79.9 67.0 %all-to-all-start.1 = ((bf16[8,128,1024]{2,1,0:T(8,128)(2,1)}), bf16[8,128,1024]{2,1,0:T(8,128)(2,1)}, u32[]{:S(2)}, u32[]{:S(2)}) async-start(bf16[8,128,1024]{2,1,0:T(8,128)(2,1)} %get-tuple-element.14), calls=%async_computation.1 | async-start | bytes 4194304 | tf_op jit(solution)/shard_map/all_to_all | solution.py:307
  146.9 66.5 %all-to-all-start.2 = ((bf16[8,128,1024]{2,1,0:T(8,128)(2,1)}), bf16[8,128,1024]{2,1,0:T(8,128)(2,1)S(1)}, u32[]{:S(2)}, u32[]{:S(2)}) async-start(bf16[8,128,1024]{2,1,0:T(8,128)(2,1)} %bitcast.22), calls=%async_computation.2 | async-start | bytes 4194304 | tf_op jit(solution)/shard_map/all_to_all | solution.py:307
  152.9 66.5 %copy-start.2 = (f32[8,1024]{1,0:T(8,128)S(1)}, f32[8,1024]{1,0:T(8,128)}, u32[]{:S(2)}) copy-start(f32[8,1024]{1,0:T(8,128)} %get-tuple-element.13) | copy-start | bytes 98308
  213.4 17.7 %copy-start = (bf16[8,128,1024]{2,1,0:T(8,128)(2,1)}, bf16[8,128,1024]{2,1,0:T(8,128)(2,1)S(1)}, u32[]{:S(2)}) copy-start(bf16[8,128,1024]{2,1,0:T(8,128)(2,1)S(1)} %all-to-all-done.2.refs_0_) | copy-start | bytes 6291460
  213.4 72.8 %all-to-all-start.3 = ((bf16[8,128,1024]{2,1,0:T(8,128)(2,1)}), bf16[8,128,1024]{2,1,0:T(8,128)(2,1)}, u32[]{:S(2)}, u32[]{:S(2)}) async-start(bf16[8,128,1024]{2,1,0:T(8,128)(2,1)} %bitcast.20), calls=%async_computation.3 | async-start | bytes 4194304 | tf_op jit(solution)/shard_map/all_to_all | solution.py:307
